TPU v7x, 128 devices: a whole 4x4x4 slice. The times are simulated.
128 devices in a mesh: obl: 16 (over y, z), scn: 8 (over x, core).
Axes of the slice: x: 4, y: 4, z: 4, core: 2. Of those that a mesh axis runs over, the one named last changes fastest.
Arguments:
- factors: bfloat16 [32768, 128], P('scn'), may hold values from -6 to 6
- idiosyncratic: bfloat16 [32768, 32768], P('obl', 'scn'), may hold values from -6 to 6
- loadings: bfloat16 [32768, 128], P('obl'), may hold values from -0.375 to 0.375
- rating: int32 [32768], P('obl'), may hold values from 0 to 15
- barrier: float32 [16], replicated, may hold values from 1 to 3
- loss_given: float32 [32768], P('obl'), may hold values from 0.2 to 0.9
- sector: int32 [32768], P('obl'), may hold values from 0 to 15, as said below
- allowed: int32 [256, 16], replicated, may hold values from 0 to 1, as said below
- holdings: float32 [32768, 256], P('obl'), may hold values from 0.1 to 10
Outputs:
- positions: float32 [32768, 256], P('obl')
- shortfall: float32 [2, 256], replicated
Inputs may be any that keep to these rules, and one draw needn't show every extreme that they name: Each sector holds exactly 2048 obligors. `allowed`: every mandate allows at least one sector.
All inputs are finite; a program needn't handle non-finite values.
Results may differ from a plain program's by a relative error of at most 0.0003.
Values may be sent and summed in bfloat16 or wider, within the bound.
No kernel may reach another device: no remote copies, remote signals or barrier semaphores. Data moves between devices by JAX's collectives and lax.ppermute only.
A program may use at most 128 MiB of HBM per device.

v0:
```python
import functools
import jax
import jax.numpy as jnp
from jax import lax
from jax.sharding import Mesh
from jax.sharding import PartitionSpec as P

STEPS = 2
OBL = ("obl_0", "obl_1")
IDIO_SCALE = 0.8
SHARP = 2.0
LEVEL = 0.99
QUANTILE = 2.326
SMOOTH = 0.5
EPSILON = 1e-06
STEP_RATE = 8.0


def one_axis_at_a_time(array, axes):
    return functools.reduce(lax.psum, axes, array)


def copy_for_each(array, axis):
    devices = lax.axis_size(axis)
    return lax.all_to_all(
        jnp.broadcast_to(array[None], (devices, *array.shape)), axis, 0, 0, tiled=True
    )


def over_copies(array, axis):
    everything = copy_for_each(array, axis)
    return jnp.sum(everything, axis=0)


def together(arrays, axis):
    vector, at, outs = (jnp.concatenate([a.reshape(-1) for a in arrays]), 0, [])
    running = over_copies(vector, axis)
    for a in arrays:
        outs.append(running[at : at + a.size].reshape(a.shape))
        at += a.size
    return tuple(outs)


def filled_up(lines, devices):
    spare = -len(lines) % devices
    return jnp.pad(lines, [(0, spare)] + [(0, 0)] * (lines.ndim - 1))


def total_of(array, axis):
    lines = array.reshape(-1, *array.shape[1:][-1:])
    own = lax.psum_scatter(
        filled_up(lines, lax.axis_size(axis)), axis, scatter_dimension=0, tiled=True
    )
    whole = lax.all_gather(own, axis).reshape(-1, *lines.shape[1:])
    return lax.slice_in_dim(whole, 0, len(lines)).reshape(array.shape)


def tail_terms(losses, center, spread, tail_scale):
    deviation = jnp.sqrt(spread + EPSILON)
    thresh = center + QUANTILE * deviation
    smooth_width = SMOOTH * deviation
    scaled = (losses - thresh) / smooth_width
    tail_weight = (jax.nn.sigmoid(scaled) * tail_scale).astype(jnp.bfloat16)
    return (scaled, thresh, smooth_width, tail_weight)


def on_device(
    factors, idiosyncratic, loadings, rating, barrier, loss_given, sector, allowed, holdings
):
    obl_dev = idiosyncratic.shape[0]
    scn_dev = idiosyncratic.shape[1]
    obligors = obl_dev * lax.axis_size(OBL)
    scenarios = scn_dev * lax.axis_size("scn")
    tail_scale = 1.0 / ((1.0 - LEVEL) * scenarios)
    sector_hot = (sector[:, None] == jnp.arange(allowed.shape[1])[None, :]).astype(jnp.float32)
    eligible = lax.dot_general(
        sector_hot,
        allowed.astype(jnp.float32),
        (((1,), (1,)), ((), ())),
        precision=lax.Precision.HIGHEST,
    )
    rating_hot = (rating[:, None] == jnp.arange(barrier.shape[0])[None, :]).astype(jnp.float32)
    barrier_rows = jnp.dot(rating_hot, barrier, precision=lax.Precision.HIGHEST)
    systematic = lax.dot_general(
        loadings, factors, (((1,), (1,)), ((), ())), preferred_element_type=jnp.float32
    )
    latent = systematic + IDIO_SCALE * idiosyncratic.astype(jnp.float32)
    default_prob = jax.nn.sigmoid((latent - barrier_rows[:, None]) * SHARP).astype(jnp.bfloat16)
    weighted = eligible * holdings
    totals = one_axis_at_a_time(jnp.sum(weighted, 0), OBL)
    positions = obligors * weighted / totals
    results = []
    for iteration in range(STEPS):
        exposure = (loss_given[:, None] * positions / obligors).astype(jnp.bfloat16)
        partial_value = lax.dot_general(
            default_prob, exposure, (((0,), (0,)), ((), ())), preferred_element_type=jnp.float32
        )
        losses = lax.psum(partial_value, OBL)
        first, second = together((jnp.sum(losses, 0), jnp.sum(losses * losses, 0)), "scn")
        center = first / scenarios
        spread = second / scenarios - center * center
        scaled, thresh, smooth_width, tail_weight = tail_terms(losses, center, spread, tail_scale)
        tail_sum = over_copies(jnp.sum(jax.nn.softplus(scaled), 0), "scn")
        results.append(thresh + smooth_width * (tail_sum * tail_scale))
        gradient = jnp.dot(default_prob, tail_weight, preferred_element_type=jnp.float32)
        gradient = total_of(gradient, "scn")
        gradient = loss_given[:, None] * eligible * gradient
        unnorm = positions * jnp.exp(-STEP_RATE * gradient)
        totals = one_axis_at_a_time(jnp.sum(unnorm, 0), OBL)
        positions = obligors * unnorm / totals
    return (positions, jnp.stack(results))


def solution(mesh):
    finer = Mesh(mesh.devices.reshape(4, 4, mesh.shape["scn"]), ("obl_0", "obl_1", "scn"))
    in_specs = (
        P("scn", None),
        P(OBL, "scn"),
        P(OBL, None),
        P(OBL),
        P(),
        P(OBL),
        P(OBL),
        P(),
        P(OBL, None),
    )
    out_specs = (P(OBL, None), P())
    return jax.shard_map(
        on_device, mesh=finer, in_specs=in_specs, out_specs=out_specs, check_vma=False
    )
```

profile of v0, /device:TPU:0, one launch (start us, length us, event | category | flops | bytes accessed | tf_op | source)
XLA Modules:
  0.0 505.9 jit_solution(1851774986560804028)
XLA Ops:
  7.2 0.0 copy-start
  7.2 0.0 copy-start.4
  7.2 0.0 copy-start.3
  7.2 0.0 all-reduce.3.cloned.1.call-start
  7.2 2.7 multiply_reduce_fusion.2
  9.9 10.9 %psum.56 = f32[256]{0:T(256)S(1)} all-reduce(f32[256]{0:T(256)S(1)} %get-tuple-element.14), channel_id=1, replica_groups=mesh['obl_0'=4,'obl_1'=4,'scn'=8] {'obl_0'}, use_global_device_ids=true, to_apply=%region_1.0 | all-reduce | flops 256 | bytes 2048 | tf_op jit(solution)/shard_map/psum | solution.py:20
  20.8 11.8 %psum.57 = f32[256]{0:T(256)S(1)} all-reduce(f32[256]{0:T(256)S(1)} %psum.56), channel_id=1, replica_groups=mesh['obl_0'=4,'obl_1'=4,'scn'=8] {'obl_1'}, use_global_device_ids=true, to_apply=%region_2.0 | all-reduce | flops 256 | bytes 2048 | tf_op jit(solution)/shard_map/psum | solution.py:20
  32.5 0.0 copy-done.3
  32.5 0.7 fusion.15
  33.3 16.5 %divide_convert_fusion = bf16[2048,4096]{1,0:T(8,128)(2,1)} fusion(bf16[2048,4096]{1,0:T(8,128)(2,1)} %param.10, f32[2048]{0:T(1024)S(1)} %bitcast.14, bf16[2048,128]{1,0:T(8,128)(2,1)} %param.11, bf16[4096,128]{1,0:T(8,128)(2,1)S(1)} %copy-done), kind=kOutput, calls=%fused_computation | convolution fusion | flops 2222981120 | bytes 35135488 | tf_op jit(solution)/shard_map/dot_general | solution.py:84
  49.8 13.6 %fusion.8 = f32[4096,256]{1,0:T(8,128)} fusion(bf16[2048,4096]{1,0:T(8,128)(2,1)} %divide_convert_fusion, f32[2048]{0:T(1024)S(1)} %copy-done.2, f32[256]{0:T(256)S(1)} %psum.57, f32[2048,256]{1,0:T(8,128)S(1)} %get-tuple-element.15, f32[2048,256]{1,0:T(8,128)} %param.17), kind=kOutput, calls=%fused_computation.24 | convolution fusion | flops 4298113024 | bytes 25175040 | tf_op jit(solution)/shard_map/dot_general | solution.py:95
  63.4 0.0 all-reduce.3.cloned.1.call-update
  63.4 0.0 reduce-scatter.3.cloned.1.call-start
  63.5 100.8 %all-reduce.3.cloned.1.call-done = f32[4096,256]{1,0:T(8,128)} async-done(((f32[4096,256]{1,0:T(8,128)}), f32[4096,256]{1,0:T(8,128)}) %all-reduce.3.cloned.1.call-update) | async-done | bytes 4194320 | tf_op jit(solution)/shard_map/psum | solution.py:98
  164.3 2.7 fusion.29
  167.0 9.4 %all_to_all.24 = f32[8,1,512]{2,1,0:T(1,128)S(1)} all-to-all(f32[8,1,512]{2,1,0:T(1,128)S(1)} %broadcast_in_dim.8), channel_id=1, replica_groups=mesh['obl_0'=4,'obl_1'=4,'scn'=8] {'scn'}, dimensions={0} | all-to-all | bytes 32768 | tf_op jit(solution)/shard_map/all_to_all | solution.py:25
  176.5 13.1 %fusion.2 = f32[2048,256]{1,0:T(8,128)} fusion(bf16[2048,4096]{1,0:T(8,128)(2,1)} %divide_convert_fusion, f32[4096,256]{1,0:T(8,128)} %all-reduce.3.cloned.1.call-done, f32[256]{0:T(256)S(1)} %broadcast_multiply_fusion.1, f32[256]{0:T(256)S(1)} %get-tuple-element.12), kind=kOutput, calls=%fused_computation.11 | convolution fusion | flops 4302307328 | bytes 23070720 | tf_op jit(solution)/shard_map/dot_general | solution.py:105
  189.6 0.0 reduce-scatter.3.cloned.1.call-update
  189.7 0.0 all-gather.5.cloned.1.call-start
  189.7 31.7 %reduce-scatter.3.cloned.1.call-done = f32[256,256]{1,0:T(8,128)} async-done(((f32[2048,256]{1,0:T(8,128)}), f32[256,256]{1,0:T(8,128)}) %reduce-scatter.3.cloned.1.call-update) | async-done | bytes 262160 | tf_op jit(solution)/shard_map/reduce_scatter | solution.py:51
  221.4 0.0 all-gather.5.cloned.1.call-update
  221.5 0.0 all-reduce.5.cloned.1.call-start
  221.5 25.9 %all-gather.5.cloned.1.call-done = f32[2048,256]{1,0:T(8,128)} async-done(((f32[256,256]{1,0:T(8,128)}), f32[2048,256]{1,0:T(8,128)}) %all-gather.5.cloned.1.call-update) | async-done | bytes 2097168 | tf_op jit(solution)/shard_map/all_gather | solution.py:54
  247.4 4.3 fusion.31
  251.7 10.4 %psum.59 = f32[256]{0:T(256)S(1)} all-reduce(f32[256]{0:T(256)S(1)} %get-tuple-element.10), channel_id=1, replica_groups=mesh['obl_0'=4,'obl_1'=4,'scn'=8] {'obl_0'}, use_global_device_ids=true, to_apply=%region_9.10 | all-reduce | flops 256 | bytes 2048 | tf_op jit(solution)/shard_map/psum | solution.py:20
  262.1 10.7 %psum.60 = f32[256]{0:T(256)S(1)} all-reduce(f32[256]{0:T(256)S(1)} %psum.59), channel_id=1, replica_groups=mesh['obl_0'=4,'obl_1'=4,'scn'=8] {'obl_1'}, use_global_device_ids=true, to_apply=%region_10.11 | all-reduce | flops 256 | bytes 2048 | tf_op jit(solution)/shard_map/psum | solution.py:20
  272.8 13.6 %fusion.9 = f32[4096,256]{1,0:T(8,128)} fusion(bf16[2048,4096]{1,0:T(8,128)(2,1)} %divide_convert_fusion, f32[2048]{0:T(1024)S(1)} %copy-done.2, f32[2048,256]{1,0:T(8,128)} %get-tuple-element.11, f32[256]{0:T(256)S(1)} %psum.60), kind=kOutput, calls=%fused_computation.25 | convolution fusion | flops 4297588736 | bytes 23077888 | tf_op jit(solution)/shard_map/dot_general | solution.py:95
  286.3 0.0 all-reduce.5.cloned.1.call-update
  286.4 0.3 reduce-scatter.5.cloned.1.call-start
  286.6 99.7 %all-reduce.5.cloned.1.call-done = f32[4096,256]{1,0:T(8,128)} async-done(((f32[4096,256]{1,0:T(8,128)}), f32[4096,256]{1,0:T(8,128)}) %all-reduce.5.cloned.1.call-update) | async-done | bytes 4194320 | tf_op jit(solution)/shard_map/psum | solution.py:98
  386.3 2.7 fusion.28
  389.1 9.4 %all_to_all.25 = f32[8,1,512]{2,1,0:T(1,128)S(1)} all-to-all(f32[8,1,512]{2,1,0:T(1,128)S(1)} %broadcast_in_dim.9), channel_id=1, replica_groups=mesh['obl_0'=4,'obl_1'=4,'scn'=8] {'scn'}, dimensions={0} | all-to-all | bytes 32768 | tf_op jit(solution)/shard_map/all_to_all | solution.py:25
  398.5 13.2 %fusion.3 = f32[2048,256]{1,0:T(8,128)} fusion(bf16[2048,4096]{1,0:T(8,128)(2,1)} %divide_convert_fusion, f32[4096,256]{1,0:T(8,128)} %all-reduce.5.cloned.1.call-done, f32[256]{0:T(256)S(1)} %broadcast_multiply_fusion, f32[256]{0:T(256)S(1)} %get-tuple-element.8), kind=kOutput, calls=%fused_computation.12 | convolution fusion | flops 4302307328 | bytes 23070720 | tf_op jit(solution)/shard_map/dot_general | solution.py:105
  411.7 0.0 reduce-scatter.5.cloned.1.call-update
  411.8 0.0 all-gather.7.cloned.1.call-start
  411.8 31.8 %reduce-scatter.5.cloned.1.call-done = f32[256,256]{1,0:T(8,128)} async-done(((f32[2048,256]{1,0:T(8,128)}), f32[256,256]{1,0:T(8,128)}) %reduce-scatter.5.cloned.1.call-update) | async-done | bytes 262160 | tf_op jit(solution)/shard_map/reduce_scatter | solution.py:51
  443.6 0.0 all-gather.7.cloned.1.call-update
  443.6 4.8 fusion
  448.4 7.7 %all_to_all.26 = f32[8,1,256]{2,1,0:T(1,128)S(1)} all-to-all(f32[8,1,256]{2,1,0:T(1,128)S(1)} %broadcast_in_dim.10), channel_id=1, replica_groups=mesh['obl_0'=4,'obl_1'=4,'scn'=8] {'scn'}, dimensions={0} | all-to-all | bytes 16384 | tf_op jit(solution)/shard_map/all_to_all | solution.py:25
  456.1 4.8 fusion.1
  460.9 0.6 broadcast_in_dim.11
  461.5 3.3 all-to-all-start.3
  464.8 5.2 %all-to-all-done.3 = f32[8,1,256]{2,1,0:T(1,128)S(1)} async-done(((f32[8,1,256]{2,1,0:T(1,128)}), f32[8,1,256]{2,1,0:T(1,128)S(1)}, u32[]{:S(2)}, u32[]{:S(2)}) %all-to-all-start.3) | async-done | bytes 8224 | tf_op jit(solution)/shard_map/all_to_all | solution.py:25
  470.0 0.6 pad_maximum_fusion.2
  470.6 4.3 fusion.30
  474.9 10.4 %psum.62 = f32[256]{0:T(256)S(1)} all-reduce(f32[256]{0:T(256)S(1)} %get-tuple-element.6), channel_id=1, replica_groups=mesh['obl_0'=4,'obl_1'=4,'scn'=8] {'obl_0'}, use_global_device_ids=true, to_apply=%region_17.18 | all-reduce | flops 256 | bytes 2048 | tf_op jit(solution)/shard_map/psum | solution.py:20
  485.4 10.7 %psum.63 = f32[256]{0:T(256)S(1)} all-reduce(f32[256]{0:T(256)S(1)} %psum.62), channel_id=1, replica_groups=mesh['obl_0'=4,'obl_1'=4,'scn'=8] {'obl_1'}, use_global_device_ids=true, to_apply=%region_18.19 | all-reduce | flops 256 | bytes 2048 | tf_op jit(solution)/shard_map/psum | solution.py:20
  496.0 3.1 multiply_divide_fusion
  (22 shorter events, 0.2 us)
Async XLA Ops:
  7.2 26.1 %copy-start = (bf16[4096,128]{1,0:T(8,128)(2,1)S(1)}, bf16[4096,128]{1,0:T(8,128)(2,1)}, u32[]{:S(2)}) copy-start(bf16[4096,128]{1,0:T(8,128)(2,1)} %param.9) | copy-start | bytes 3145732
  7.2 25.3 %copy-start.4 = (f32[16]{0:T(128)S(1)}, f32[16]{0:T(128)}, u32[]{:S(2)}) copy-start(f32[16]{0:T(128)} %param.13) | copy-start | bytes 196
  7.2 25.3 %copy-start.3 = (s32[2048]{0:T(1024)S(1)}, s32[2048]{0:T(1024)}, u32[]{:S(2)}) copy-start(s32[2048]{0:T(1024)} %param.12) | copy-start | bytes 24580
  7.2 157.1 %all-reduce.3.cloned.1.call-start = ((), (), s32[]{:S(2)}) async-start(), calls=%async_computation.6 | async-start | bytes 8388608 | tf_op jit(solution)/shard_map/psum | solution.py:98
  33.2 16.5 %copy-start.2 = (f32[2048]{0:T(1024)S(1)}, f32[2048]{0:T(1024)}, u32[]{:S(2)}) copy-start(f32[2048]{0:T(1024)} %param.14) | copy-start | bytes 24580
  63.4 158.0 %reduce-scatter.3.cloned.1.call-start = ((), (), s32[]{:S(2)}) async-start(), calls=%async_computation.7 | async-start | bytes 2359296 | tf_op jit(solution)/shard_map/reduce_scatter | solution.py:51
  189.7 57.7 %all-gather.5.cloned.1.call-start = ((), (), s32[]{:S(2)}) async-start(), calls=%async_computation.10 | async-start | bytes 2359296 | tf_op jit(solution)/shard_map/all_gather | solution.py:54
  221.5 164.8 %all-reduce.5.cloned.1.call-start = ((), (), s32[]{:S(2)}) async-start(), calls=%async_computation.8 | async-start | bytes 8388608 | tf_op jit(solution)/shard_map/psum | solution.py:98
  286.4 157.3 %reduce-scatter.5.cloned.1.call-start = ((), (), s32[]{:S(2)}) async-start(), calls=%async_computation.9 | async-start | bytes 2359296 | tf_op jit(solution)/shard_map/reduce_scatter | solution.py:51
  411.8 58.9 %all-gather.7.cloned.1.call-start = ((), (), s32[]{:S(2)}) async-start(), calls=%async_computation.11 | async-start | bytes 2359296 | tf_op jit(solution)/shard_map/all_gather | solution.py:54
  461.5 8.5 %all-to-all-start.3 = ((f32[8,1,256]{2,1,0:T(1,128)}), f32[8,1,256]{2,1,0:T(1,128)S(1)}, u32[]{:S(2)}, u32[]{:S(2)}) async-start(f32[8,1,256]{2,1,0:T(1,128)} %broadcast_in_dim.11), calls=%async_computation.5 | async-start | bytes 16384 | tf_op jit(solution)/shard_map/all_to_all | solution.py:25
  470.6 28.5 %copy-start.1 = (bf16[4096,128]{1,0:T(8,128)(2,1)S(1)}, bf16[4096,128]{1,0:T(8,128)(2,1)}, u32[]{:S(2)}) copy-start(bf16[4096,128]{1,0:T(8,128)(2,1)} %param.9) | copy-start | bytes 3145732
Sparse Core Ops, SparseCore 0:
  63.5 100.6 all-reduce.2
  189.8 31.5 reduce-scatter.2
  223.2 24.1 all-gather.4
  286.5 99.7 all-reduce.4
  411.9 31.6 reduce-scatter.4
  445.2 24.0 all-gather.6
where the time goes:
time: 507 us; the launch traced here: 506 us
  waiting for transfers between devices  295 us (58%)
  blocking collectives  91.3 us (18%)
  matrix products  73.4 us (14%)
  other arithmetic  27.4 us (5%)
  between operations  14.2 us (3%)
    psum x2, waiting for transfers between devices, on_device(): losses = lax.psum(partial_value, OBL)  200 us
    psum x6, blocking collectives, one_axis_at_a_time(): return functools.reduce(lax.psum, axes, array)  64.8 us
    reduce_scatter x2, waiting for transfers between devices, total_of(): lax.psum_scatter(filled_up(lines, lax.axis_size(axis)), axis, scatter_dim...  63.5 us
    dot_general x2, matrix products, on_device(): lax.dot_general(default_prob, exposure, (((0,), (0,)), ((), ())), preferr...  27.2 us
    all_to_all x3, blocking collectives, copy_for_each(): lax.all_to_all(jnp.broadcast_to(array[None], (devices, *array.shape)), ax...  26.5 us
    dot_general x2, matrix products, on_device(): jnp.dot(default_prob, tail_weight, preferred_element_type=jnp.float32)  26.4 us
    all_gather x2, waiting for transfers between devices, total_of(): whole = lax.all_gather(own, axis).reshape(-1, *lines.shape[1:])  25.9 us
    dot_general x1, matrix products, on_device(): lax.dot_general(loadings, factors, (((1,), (1,)), ((), ())), preferred_el...  16.5 us
  transfers between devices with their start and end apart: 7, of which 6 were waited for; matrix products, arithmetic and copies ran while one was open for 2% of the time, Pallas kernels for 0%

commit v1 on v0

--- a/solution.py
+++ b/solution.py
@@ -95,7 +95,7 @@
         partial_value = lax.dot_general(
             default_prob, exposure, (((0,), (0,)), ((), ())), preferred_element_type=jnp.float32
         )
-        losses = lax.psum(partial_value, OBL)
+        losses = lax.psum(lax.psum(partial_value, "obl_0"), "obl_1")
         first, second = together((jnp.sum(losses, 0), jnp.sum(losses * losses, 0)), "scn")
         center = first / scenarios
         spread = second / scenarios - center * center

time: 507 us -> 675 us (1.33)
  waiting for transfers between devices: 295 us -> 463 us
    psum x2 -> x4, waiting for transfers between devices: 200 us -> 369 us  [on_device(): losses = lax.psum(lax.psum(partial_value, 'obl_0'), 'obl_1')]
  transfers between devices with their start and end apart: 7 -> 9, of which waited for: 6 -> 8; matrix products, arithmetic and copies ran while one was open for 2% -> 2% of each run, Pallas kernels for 0% -> 0%
where the time goes in v1:
time: 675 us; the launch traced here: 674 us
  waiting for transfers between devices  463 us (69%)
  blocking collectives  91.3 us (14%)
  matrix products  73.4 us (11%)
  other arithmetic  27.4 us (4%)
  between operations  14.2 us (2%)
    psum x4, waiting for transfers between devices, on_device(): losses = lax.psum(lax.psum(partial_value, 'obl_0'), 'obl_1')  369 us
    psum x6, blocking collectives, one_axis_at_a_time(): return functools.reduce(lax.psum, axes, array)  64.8 us
    reduce_scatter x2, waiting for transfers between devices, total_of(): lax.psum_scatter(filled_up(lines, lax.axis_size(axis)), axis, scatter_dim...  63.8 us
    dot_general x2, matrix products, on_device(): lax.dot_general(default_prob, exposure, (((0,), (0,)), ((), ())), preferr...  27.1 us
    all_to_all x3, blocking collectives, copy_for_each(): lax.all_to_all(jnp.broadcast_to(array[None], (devices, *array.shape)), ax...  26.5 us
    dot_general x2, matrix products, on_device(): jnp.dot(default_prob, tail_weight, preferred_element_type=jnp.float32)  26.4 us
    all_gather x2, waiting for transfers between devices, total_of(): whole = lax.all_gather(own, axis).reshape(-1, *lines.shape[1:])  25.5 us
    dot_general x1, matrix products, on_device(): lax.dot_general(loadings, factors, (((1,), (1,)), ((), ())), preferred_el...  16.5 us
  transfers between devices with their start and end apart: 9, of which 8 were waited for; matrix products, arithmetic and copies ran while one was open for 2% of the time, Pallas kernels for 0%

profile of v1, /device:TPU:0, one launch (start us, length us, event | category | flops | bytes accessed | tf_op | source)
XLA Modules:
  0.0 674.1 jit_solution(10769971168835517912)
XLA Ops:
  7.2 0.0 all-reduce.5.cloned.1.call-start
  7.2 2.7 multiply_reduce_fusion.2
  9.9 10.9 %psum.70 = f32[256]{0:T(256)S(1)} all-reduce(f32[256]{0:T(256)S(1)} %get-tuple-element.14), channel_id=1, replica_groups=mesh['obl_0'=4,'obl_1'=4,'scn'=8] {'obl_0'}, use_global_device_ids=true, to_apply=%region_1.0 | all-reduce | flops 256 | bytes 2048 | tf_op jit(solution)/shard_map/psum | solution.py:20
  20.8 11.8 %psum.71 = f32[256]{0:T(256)S(1)} all-reduce(f32[256]{0:T(256)S(1)} %psum.70), channel_id=1, replica_groups=mesh['obl_0'=4,'obl_1'=4,'scn'=8] {'obl_1'}, use_global_device_ids=true, to_apply=%region_2.0 | all-reduce | flops 256 | bytes 2048 | tf_op jit(solution)/shard_map/psum | solution.py:20
  32.5 0.7 fusion.15
  33.3 16.5 %divide_convert_fusion = bf16[2048,4096]{1,0:T(8,128)(2,1)} fusion(bf16[2048,4096]{1,0:T(8,128)(2,1)} %param.10, f32[2048]{0:T(1024)S(1)} %bitcast.14, bf16[2048,128]{1,0:T(8,128)(2,1)} %param.11, bf16[4096,128]{1,0:T(8,128)(2,1)S(1)} %copy-done), kind=kOutput, calls=%fused_computation | convolution fusion | flops 2222981120 | bytes 35135488 | tf_op jit(solution)/shard_map/dot_general | solution.py:84
  49.8 13.6 %fusion.8 = f32[4096,256]{1,0:T(8,128)} fusion(bf16[2048,4096]{1,0:T(8,128)(2,1)} %divide_convert_fusion, f32[2048]{0:T(1024)S(1)} %copy-done.2, f32[256]{0:T(256)S(1)} %psum.71, f32[2048,256]{1,0:T(8,128)S(1)} %get-tuple-element.15, f32[2048,256]{1,0:T(8,128)} %param.17), kind=kOutput, calls=%fused_computation.24 | convolution fusion | flops 4298113024 | bytes 25175040 | tf_op jit(solution)/shard_map/dot_general | solution.py:95
  63.3 0.0 all-reduce.5.cloned.1.call-update
  63.4 0.0 all-reduce.7.cloned.1.call-start
  63.4 89.7 %all-reduce.5.cloned.1.call-done = f32[4096,256]{1,0:T(8,128)} async-done(((f32[4096,256]{1,0:T(8,128)}), f32[4096,256]{1,0:T(8,128)}) %all-reduce.5.cloned.1.call-update) | async-done | bytes 4194320 | tf_op jit(solution)/shard_map/psum | solution.py:98
  153.1 0.0 all-reduce.7.cloned.1.call-update
  153.2 0.0 reduce-scatter.3.cloned.1.call-start
  153.2 95.2 %all-reduce.7.cloned.1.call-done = f32[4096,256]{1,0:T(8,128)} async-done(((f32[4096,256]{1,0:T(8,128)}), f32[4096,256]{1,0:T(8,128)}) %all-reduce.7.cloned.1.call-update) | async-done | bytes 4194320 | tf_op jit(solution)/shard_map/psum | solution.py:98
  248.4 2.7 fusion.29
  251.2 9.4 %all_to_all.24 = f32[8,1,512]{2,1,0:T(1,128)S(1)} all-to-all(f32[8,1,512]{2,1,0:T(1,128)S(1)} %broadcast_in_dim.8), channel_id=1, replica_groups=mesh['obl_0'=4,'obl_1'=4,'scn'=8] {'scn'}, dimensions={0} | all-to-all | bytes 32768 | tf_op jit(solution)/shard_map/all_to_all | solution.py:25
  260.7 13.1 %fusion.2 = f32[2048,256]{1,0:T(8,128)} fusion(bf16[2048,4096]{1,0:T(8,128)(2,1)} %divide_convert_fusion, f32[4096,256]{1,0:T(8,128)} %all-reduce.7.cloned.1.call-done, f32[256]{0:T(256)S(1)} %broadcast_multiply_fusion.1, f32[256]{0:T(256)S(1)} %get-tuple-element.12), kind=kOutput, calls=%fused_computation.11 | convolution fusion | flops 4302307328 | bytes 23070720 | tf_op jit(solution)/shard_map/dot_general | solution.py:105
  273.8 0.0 reduce-scatter.3.cloned.1.call-update
  273.8 0.0 all-gather.5.cloned.1.call-start
  273.9 31.9 %reduce-scatter.3.cloned.1.call-done = f32[256,256]{1,0:T(8,128)} async-done(((f32[2048,256]{1,0:T(8,128)}), f32[256,256]{1,0:T(8,128)}) %reduce-scatter.3.cloned.1.call-update) | async-done | bytes 262160 | tf_op jit(solution)/shard_map/reduce_scatter | solution.py:51
  305.8 0.0 all-gather.5.cloned.1.call-update
  305.8 0.0 all-reduce.9.cloned.1.call-start
  305.8 25.5 %all-gather.5.cloned.1.call-done = f32[2048,256]{1,0:T(8,128)} async-done(((f32[256,256]{1,0:T(8,128)}), f32[2048,256]{1,0:T(8,128)}) %all-gather.5.cloned.1.call-update) | async-done | bytes 2097168 | tf_op jit(solution)/shard_map/all_gather | solution.py:54
  331.4 4.3 fusion.31
  335.7 10.4 %psum.74 = f32[256]{0:T(256)S(1)} all-reduce(f32[256]{0:T(256)S(1)} %get-tuple-element.10), channel_id=1, replica_groups=mesh['obl_0'=4,'obl_1'=4,'scn'=8] {'obl_0'}, use_global_device_ids=true, to_apply=%region_10.11 | all-reduce | flops 256 | bytes 2048 | tf_op jit(solution)/shard_map/psum | solution.py:20
  346.1 10.7 %psum.75 = f32[256]{0:T(256)S(1)} all-reduce(f32[256]{0:T(256)S(1)} %psum.74), channel_id=1, replica_groups=mesh['obl_0'=4,'obl_1'=4,'scn'=8] {'obl_1'}, use_global_device_ids=true, to_apply=%region_11.12 | all-reduce | flops 256 | bytes 2048 | tf_op jit(solution)/shard_map/psum | solution.py:20
  356.8 13.6 %fusion.9 = f32[4096,256]{1,0:T(8,128)} fusion(bf16[2048,4096]{1,0:T(8,128)(2,1)} %divide_convert_fusion, f32[2048]{0:T(1024)S(1)} %copy-done.2, f32[2048,256]{1,0:T(8,128)} %get-tuple-element.11, f32[256]{0:T(256)S(1)} %psum.75), kind=kOutput, calls=%fused_computation.25 | convolution fusion | flops 4297588736 | bytes 23077888 | tf_op jit(solution)/shard_map/dot_general | solution.py:95
  370.3 0.0 all-reduce.11.cloned.1.call-start
  370.4 88.8 %all-reduce.9.cloned.1.call-done = f32[4096,256]{1,0:T(8,128)} async-done(((f32[4096,256]{1,0:T(8,128)}), f32[4096,256]{1,0:T(8,128)}) %all-reduce.9.cloned.1.call-update) | async-done | bytes 4194320 | tf_op jit(solution)/shard_map/psum | solution.py:98
  459.2 0.0 all-reduce.11.cloned.1.call-update
  459.2 0.3 reduce-scatter.5.cloned.1.call-start
  459.5 94.9 %all-reduce.11.cloned.1.call-done = f32[4096,256]{1,0:T(8,128)} async-done(((f32[4096,256]{1,0:T(8,128)}), f32[4096,256]{1,0:T(8,128)}) %all-reduce.11.cloned.1.call-update) | async-done | bytes 4194320 | tf_op jit(solution)/shard_map/psum | solution.py:98
  554.4 2.7 fusion.28
  557.2 9.4 %all_to_all.25 = f32[8,1,512]{2,1,0:T(1,128)S(1)} all-to-all(f32[8,1,512]{2,1,0:T(1,128)S(1)} %broadcast_in_dim.9), channel_id=1, replica_groups=mesh['obl_0'=4,'obl_1'=4,'scn'=8] {'scn'}, dimensions={0} | all-to-all | bytes 32768 | tf_op jit(solution)/shard_map/all_to_all | solution.py:25
  566.6 13.2 %fusion.3 = f32[2048,256]{1,0:T(8,128)} fusion(bf16[2048,4096]{1,0:T(8,128)(2,1)} %divide_convert_fusion, f32[4096,256]{1,0:T(8,128)} %all-reduce.11.cloned.1.call-done, f32[256]{0:T(256)S(1)} %broadcast_multiply_fusion, f32[256]{0:T(256)S(1)} %get-tuple-element.8), kind=kOutput, calls=%fused_computation.12 | convolution fusion | flops 4302307328 | bytes 23070720 | tf_op jit(solution)/shard_map/dot_general | solution.py:105
  579.8 0.0 reduce-scatter.5.cloned.1.call-update
  579.9 0.0 all-gather.7.cloned.1.call-start
  579.9 31.9 %reduce-scatter.5.cloned.1.call-done = f32[256,256]{1,0:T(8,128)} async-done(((f32[2048,256]{1,0:T(8,128)}), f32[256,256]{1,0:T(8,128)}) %reduce-scatter.5.cloned.1.call-update) | async-done | bytes 262160 | tf_op jit(solution)/shard_map/reduce_scatter | solution.py:51
  611.8 4.8 fusion
  616.6 7.7 %all_to_all.26 = f32[8,1,256]{2,1,0:T(1,128)S(1)} all-to-all(f32[8,1,256]{2,1,0:T(1,128)S(1)} %broadcast_in_dim.10), channel_id=1, replica_groups=mesh['obl_0'=4,'obl_1'=4,'scn'=8] {'scn'}, dimensions={0} | all-to-all | bytes 16384 | tf_op jit(solution)/shard_map/all_to_all | solution.py:25
  624.3 4.8 fusion.1
  629.1 0.6 broadcast_in_dim.11
  629.7 3.3 all-to-all-start.3
  633.0 5.2 all-to-all-done.3
  638.2 0.6 pad_maximum_fusion.2
  638.8 4.3 fusion.30
  643.1 10.4 %psum.78 = f32[256]{0:T(256)S(1)} all-reduce(f32[256]{0:T(256)S(1)} %get-tuple-element.6), channel_id=1, replica_groups=mesh['obl_0'=4,'obl_1'=4,'scn'=8] {'obl_0'}, use_global_device_ids=true, to_apply=%region_19.20 | all-reduce | flops 256 | bytes 2048 | tf_op jit(solution)/shard_map/psum | solution.py:20
  653.5 10.8 %psum.79 = f32[256]{0:T(256)S(1)} all-reduce(f32[256]{0:T(256)S(1)} %psum.78), channel_id=1, replica_groups=mesh['obl_0'=4,'obl_1'=4,'scn'=8] {'obl_1'}, use_global_device_ids=true, to_apply=%region_20.21 | all-reduce | flops 256 | bytes 2048 | tf_op jit(solution)/shard_map/psum | solution.py:20
  664.2 3.1 multiply_divide_fusion
  (28 shorter events, 0.3 us)
Async XLA Ops:
  7.2 26.1 %copy-start = (bf16[4096,128]{1,0:T(8,128)(2,1)S(1)}, bf16[4096,128]{1,0:T(8,128)(2,1)}, u32[]{:S(2)}) copy-start(bf16[4096,128]{1,0:T(8,128)(2,1)} %param.9) | copy-start | bytes 3145732
  7.2 25.3 %copy-start.4 = (f32[16]{0:T(128)S(1)}, f32[16]{0:T(128)}, u32[]{:S(2)}) copy-start(f32[16]{0:T(128)} %param.13) | copy-start | bytes 196
  7.2 25.3 %copy-start.3 = (s32[2048]{0:T(1024)S(1)}, s32[2048]{0:T(1024)}, u32[]{:S(2)}) copy-start(s32[2048]{0:T(1024)} %param.12) | copy-start | bytes 24580
  7.2 145.9 %all-reduce.5.cloned.1.call-start = ((), (), s32[]{:S(2)}) async-start(), calls=%async_computation.6 | async-start | bytes 8388608 | tf_op jit(solution)/shard_map/psum | solution.py:98
  33.2 16.5 %copy-start.2 = (f32[2048]{0:T(1024)S(1)}, f32[2048]{0:T(1024)}, u32[]{:S(2)}) copy-start(f32[2048]{0:T(1024)} %param.14) | copy-start | bytes 24580
  63.4 185.1 %all-reduce.7.cloned.1.call-start = ((), (), s32[]{:S(2)}) async-start(), calls=%async_computation.7 | async-start | bytes 8388608 | tf_op jit(solution)/shard_map/psum | solution.py:98
  153.2 152.6 %reduce-scatter.3.cloned.1.call-start = ((), (), s32[]{:S(2)}) async-start(), calls=%async_computation.8 | async-start | bytes 2359296 | tf_op jit(solution)/shard_map/reduce_scatter | solution.py:51
  273.8 57.5 %all-gather.5.cloned.1.call-start = ((), (), s32[]{:S(2)}) async-start(), calls=%async_computation.12 | async-start | bytes 2359296 | tf_op jit(solution)/shard_map/all_gather | solution.py:54
  305.8 153.4 %all-reduce.9.cloned.1.call-start = ((), (), s32[]{:S(2)}) async-start(), calls=%async_computation.9 | async-start | bytes 8388608 | tf_op jit(solution)/shard_map/psum | solution.py:98
  370.3 184.0 %all-reduce.11.cloned.1.call-start = ((), (), s32[]{:S(2)}) async-start(), calls=%async_computation.10 | async-start | bytes 8388608 | tf_op jit(solution)/shard_map/psum | solution.py:98
  459.2 152.5 %reduce-scatter.5.cloned.1.call-start = ((), (), s32[]{:S(2)}) async-start(), calls=%async_computation.11 | async-start | bytes 2359296 | tf_op jit(solution)/shard_map/reduce_scatter | solution.py:51
  579.9 58.9 %all-gather.7.cloned.1.call-start = ((), (), s32[]{:S(2)}) async-start(), calls=%async_computation.13 | async-start | bytes 2359296 | tf_op jit(solution)/shard_map/all_gather | solution.py:54
  629.7 8.5 %all-to-all-start.3 = ((f32[8,1,256]{2,1,0:T(1,128)}), f32[8,1,256]{2,1,0:T(1,128)S(1)}, u32[]{:S(2)}, u32[]{:S(2)}) async-start(f32[8,1,256]{2,1,0:T(1,128)} %broadcast_in_dim.11), calls=%async_computation.5 | async-start | bytes 16384 | tf_op jit(solution)/shard_map/all_to_all | solution.py:25
  638.8 28.5 %copy-start.1 = (bf16[4096,128]{1,0:T(8,128)(2,1)S(1)}, bf16[4096,128]{1,0:T(8,128)(2,1)}, u32[]{:S(2)}) copy-start(bf16[4096,128]{1,0:T(8,128)(2,1)} %param.9) | copy-start | bytes 3145732
Sparse Core Ops, SparseCore 0:
  63.5 89.6 all-reduce.4
  155.5 92.8 all-reduce.6
  274.0 31.7 reduce-scatter.2
  307.3 23.9 all-gather.4
  370.5 88.7 all-reduce.8
  461.4 92.8 all-reduce.10
  580.0 31.7 reduce-scatter.4
  613.5 24.0 all-gather.6
